TPU v7x, 32 devices: a whole 2x2x4 slice. The times are simulated.
32 devices in a mesh: scene: 2 (over y), pulse: 8 (over z, x), scat: 2 (over core).
Axes of the slice: x: 2, y: 2, z: 4, core: 2. Of those that a mesh axis runs over, the one named last changes fastest.
Arguments:
- positions: float32 [32768], P(('scene', 'scat')), parts along dimension 0, may hold values from -1000 to 1000
- amplitude: float32 [2, 32768], P(None, ('scene', 'scat')), parts along dimension 1, may hold values from -3 to 3
- range_cells: int32 [32768], P(('scene', 'scat')), parts along dimension 0, may hold values from 0 to 1007
- bounce: int32 [32768], P(('scene', 'scat')), parts along dimension 0, may hold values 0 or 1
- stolt_block: int32 [512, 32], P(('pulse', 'scat')), may hold values from 0 to 30
- kernel_choice: int32 [512, 32], P(('pulse', 'scat')), may hold values from 0 to 15
- kernel_bank: float32 [16, 256, 128], replicated, may hold values from -0.375 to 0.375
Outputs:
- image: float32 [2, 1024, 4096], P(None, 'scene', ('pulse', 'scat')), parts along dimension 1
There are 2 independent parts, one for each index of `scene`. A program takes and returns all parts, laid end to end along the dimension named above; an argument that names none is the same for every part. Nothing has to cross between parts.
All inputs are finite; a program needn't handle non-finite values. No bound on the sum of `bounce` on one device may be relied on, other than what follows from the above.
Results may differ from a plain program's by a relative error of at most 0.0003.
Values sent between devices are 32-bit elements; how exact they have to be, the bound alone decides.
A program may use at most 64 MiB of HBM per device.

v0:
```python
import jax
import jax.numpy as jnp
from jax import lax
from jax.sharding import PartitionSpec as P

P_SIZE = 512
SPECTRAL_BIN_LEN = 4096
B = 1024
SHIFT = 16
STOLT = 128
BLOCKS = 32


wavelength = 0.03125
spacing = 2.0
near_range = 700000.0
cell_size = 1.0
center_radio_tone = 9600000000.0
pulse_slope_rate = 150000000.0
wave_propagation_velocity = 300000000.0
highest_frequency = lax.Precision.HIGHEST


def tables(modulus, row_ids, matrix_slot_numbers):
    product = row_ids[:, None] * matrix_slot_numbers[None, :] % modulus
    angle = 2.0 * jnp.pi / modulus * product.astype(jnp.float32)
    return (jnp.cos(angle), jnp.sin(angle))


def steering(positions, amplitude, target, bounce, pulse_ids):
    along_track = (pulse_ids.astype(jnp.float32) - P_SIZE // 2) * spacing
    slant_range = near_range + cell_size * target.astype(jnp.float32)
    offset = along_track[:, None] - positions[None, :]
    excess = offset * offset / (jnp.sqrt(slant_range * slant_range + offset * offset) + slant_range)
    phase_angle = -4.0 * jnp.pi / wavelength * excess
    bounce_sign = 1.0 - 2.0 * bounce.astype(jnp.float32)
    real_part = bounce_sign * amplitude[0]
    imag_part = bounce_sign * amplitude[1]
    cos_part = jnp.cos(phase_angle)
    sin_part = jnp.sin(phase_angle)
    return (
        real_part * cos_part - imag_part * sin_part,
        real_part * sin_part + imag_part * cos_part,
    )


def binning(steer_re, guiding_phasor_quadrature, target):
    stacked = jnp.concatenate([steer_re, guiding_phasor_quadrature], axis=0).T
    return jax.ops.segment_sum(stacked, target, num_segments=B)


def echo_rows(binned, freq_ids):
    half_rows = binned.shape[1] // 2
    real_part = binned[:, :half_rows].T
    imag_part = binned[:, half_rows:].T
    left_matrix = jnp.concatenate(
        [jnp.concatenate([real_part, imag_part], 1), jnp.concatenate([imag_part, -real_part], 1)], 0
    )
    cell_ids = jnp.arange(B, dtype=jnp.int32)

    def one_block(block_ids):
        cos_part, sin_part = tables(SPECTRAL_BIN_LEN, cell_ids, block_ids)
        right_matrix = jnp.concatenate([cos_part, sin_part], 0)
        return jnp.dot(
            left_matrix,
            right_matrix,
            precision=highest_frequency,
            preferred_element_type=jnp.float32,
        )

    blocked = lax.map(one_block, freq_ids.reshape(8, -1))
    joined = blocked.transpose(1, 0, 2).reshape(2 * half_rows, -1)
    return joined.reshape(2, half_rows, -1)


def reference_phase(row_ids, matrix_slot_numbers):
    centered = (row_ids + P_SIZE // 2) % P_SIZE - P_SIZE // 2
    along_k = 2.0 * jnp.pi / (P_SIZE * spacing) * centered.astype(jnp.float32)
    slant_spatial_radian_rate = (
        4.0
        * jnp.pi
        / wave_propagation_velocity
        * (
            center_radio_tone
            + (matrix_slot_numbers.astype(jnp.float32) - SPECTRAL_BIN_LEN // 2)
            * (pulse_slope_rate / SPECTRAL_BIN_LEN)
        )
    )
    squared = along_k * along_k
    depth = near_range + cell_size * (B // 2)
    return (
        -depth
        * squared[:, None]
        / (
            jnp.sqrt(
                slant_spatial_radian_rate[None, :] * slant_spatial_radian_rate[None, :]
                - squared[:, None]
            )
            + slant_spatial_radian_rate[None, :]
        )
    )


def stolt(az_rows, first_blocks, kinds, kernel_bank):
    row_count = az_rows.shape[1]
    tiled = az_rows.reshape(2, row_count, BLOCKS, STOLT)
    windows = jnp.concatenate([tiled[:, :, :-1], tiled[:, :, 1:]], axis=3)

    def one_row(row_item):
        row_windows, firsts, chosen_kinds = row_item
        chosen = row_windows[:, firsts, :]
        kernels = kernel_bank[chosen_kinds]
        result = jnp.einsum("cbu,but->cbt", chosen, kernels, precision=highest_frequency)
        return result.reshape(2, SPECTRAL_BIN_LEN)

    output = lax.map(one_row, (windows.transpose(1, 0, 2, 3), first_blocks, kinds))
    return output.transpose(1, 0, 2)


def range_inverse(signal):
    row_count = signal.shape[1]
    long_len = 128
    short_len = SPECTRAL_BIN_LEN // long_len
    shaped = signal.reshape(2, row_count, short_len, long_len)
    short_ids = jnp.arange(short_len, dtype=jnp.int32)
    long_ids = jnp.arange(long_len, dtype=jnp.int32)
    cosine_first_term, sin_one = tables(short_len, short_ids, short_ids)
    step_re = jnp.einsum(
        "kf,rfg->rkg", cosine_first_term, shaped[0], precision=highest_frequency
    ) - jnp.einsum("kf,rfg->rkg", sin_one, shaped[1], precision=highest_frequency)
    step_im = jnp.einsum(
        "kf,rfg->rkg", cosine_first_term, shaped[1], precision=highest_frequency
    ) + jnp.einsum("kf,rfg->rkg", sin_one, shaped[0], precision=highest_frequency)
    cos_twist, sin_twist = tables(SPECTRAL_BIN_LEN, short_ids, long_ids)
    twist_re = step_re * cos_twist - step_im * sin_twist
    twist_imaginary = step_re * sin_twist + step_im * cos_twist
    cos_two, sin_two = tables(long_len, long_ids, long_ids)
    final_re = jnp.einsum(
        "rkg,gh->rkh", twist_re, cos_two, precision=highest_frequency
    ) - jnp.einsum("rkg,gh->rkh", twist_imaginary, sin_two, precision=highest_frequency)
    final_im = jnp.einsum(
        "rkg,gh->rkh", twist_re, sin_two, precision=highest_frequency
    ) + jnp.einsum("rkg,gh->rkh", twist_imaginary, cos_two, precision=highest_frequency)
    final_re = final_re.transpose(0, 2, 1).reshape(row_count, SPECTRAL_BIN_LEN) / SPECTRAL_BIN_LEN
    final_im = final_im.transpose(0, 2, 1).reshape(row_count, SPECTRAL_BIN_LEN) / SPECTRAL_BIN_LEN
    return jnp.stack([final_re, final_im])


def on_device(positions, amplitude, range_cells, bounce, stolt_block, kernel_choice, kernel_bank):
    n_pulse = lax.axis_size("pulse")
    n_scat = lax.axis_size("scat")
    pulse_here = lax.axis_index("pulse")
    scat_here = lax.axis_index("scat")
    per_pulse = P_SIZE // n_pulse
    block_width = SPECTRAL_BIN_LEN // (n_pulse * n_scat)
    pulse_ids = pulse_here * per_pulse + jnp.arange(per_pulse, dtype=jnp.int32)
    target = range_cells + SHIFT * bounce
    block_ids = jnp.arange(n_pulse, dtype=jnp.int32)[:, None] * n_scat + scat_here
    owned_freqs = (
        block_ids * block_width + jnp.arange(block_width, dtype=jnp.int32)[None, :]
    ).reshape(-1)
    steer_re, guiding_phasor_quadrature = steering(positions, amplitude, target, bounce, pulse_ids)
    binned = lax.psum(binning(steer_re, guiding_phasor_quadrature, target), "scat")
    owned_echo = echo_rows(binned, owned_freqs)
    turned = lax.all_to_all(owned_echo, "pulse", split_axis=2, concat_axis=1, tiled=True)
    all_ids = jnp.arange(P_SIZE, dtype=jnp.int32)
    cos_az, sin_az = tables(P_SIZE, all_ids, all_ids)
    flattened = jnp.concatenate([turned[0], turned[1]], axis=1)
    product = jnp.dot(
        jnp.concatenate([cos_az, sin_az], 0),
        flattened,
        precision=highest_frequency,
        preferred_element_type=jnp.float32,
    )
    spec_re = product[:P_SIZE, :block_width] + product[P_SIZE:, block_width:]
    spec_im = product[:P_SIZE, block_width:] - product[P_SIZE:, :block_width]
    freq_here = (pulse_here * n_scat + scat_here) * block_width + jnp.arange(
        block_width, dtype=jnp.int32
    )
    phase_angle = reference_phase(all_ids, freq_here)
    cos_ref = jnp.cos(phase_angle)
    sin_ref = jnp.sin(phase_angle)
    spectrum = jnp.stack(
        [spec_re * cos_ref - spec_im * sin_ref, spec_re * sin_ref + spec_im * cos_ref]
    )
    az_rows = lax.all_to_all(spectrum, ("pulse", "scat"), split_axis=1, concat_axis=2, tiled=True)
    stolted = stolt(az_rows, stolt_block, kernel_choice, kernel_bank)
    ranged = range_inverse(stolted)
    columns = lax.all_to_all(ranged, ("pulse", "scat"), split_axis=2, concat_axis=1, tiled=True)
    cos_inv, sin_inv = tables(P_SIZE, all_ids, all_ids)
    flat_columns = jnp.concatenate([columns[0], columns[1]], axis=1)
    final = jnp.dot(
        jnp.concatenate([cos_inv, sin_inv], 0),
        flat_columns,
        precision=highest_frequency,
        preferred_element_type=jnp.float32,
    )
    image_re = (final[:P_SIZE, :block_width] - final[P_SIZE:, block_width:]) / P_SIZE
    image_im = (final[:P_SIZE, block_width:] + final[P_SIZE:, :block_width]) / P_SIZE
    return jnp.stack([image_re, image_im])


def solution(mesh):
    placed = (
        P(("scene", "scat")),
        P(None, ("scene", "scat")),
        P(("scene", "scat")),
        P(("scene", "scat")),
        P(("pulse", "scat"), None),
        P(("pulse", "scat"), None),
        P(),
    )
    return jax.shard_map(
        on_device,
        mesh=mesh,
        in_specs=placed,
        out_specs=P(None, "scene", ("pulse", "scat")),
        check_vma=False,
    )
```

profile of v0, /device:TPU:1, one launch (start us, length us, event | category | flops | bytes accessed | tf_op | source)
XLA Modules:
  0.0 652.9 jit_solution(5601774817201870389)
XLA Ops:
  8.4 9.4 %multiply_subtract_fusion = (f32[64,8192]{1,0:T(8,128)S(1)}, f32[64,8192]{1,0:T(8,128)S(1)}) fusion(f32[8192]{0:T(1024)S(1)} %get-tuple-element.208, f32[8192]{0:T(1024)S(1)} %convert_add_fusion, f32[8192]{0:T(1024)S(1)} %get-tuple-element.209, f32[8192]{0:T(1024)} %param.11, f32[64]{0:T(128)S(1)} %add_multiply_fusion.1, f32[8192]{0:T(1024)S(1)} %get-tuple-element.207), kind=kLoop, calls=%fused_computation.42 | loop fusion | flops 6291456 | bytes 4358400 | tf_op jit(solution)/shard_map/sub | solution.py:42
  20.1 5.6 copy.48
  25.8 45.3 %scatter_custom_fusion = f32[1024,128]{1,0:T(8,128)} fusion(s32[8192]{0:T(1024)S(1)} %get-tuple-element.210, f32[8192,128]{1,0:T(8,128)} %copy.48, f32[]{:T(128)} %constant.163.clone.1), kind=kCustom, calls=%fused_computation.97 | custom fusion | flops 1048576 | bytes 524800 | tf_op jit(solution)/shard_map/scatter-add | solution.py:49
  71.2 21.1 %all-reduce.2.cloned.1.call-done = f32[1024,128]{1,0:T(8,128)} async-done(((f32[1024,128]{1,0:T(8,128)}), f32[1024,128]{1,0:T(8,128)}) %all-reduce.2.cloned.1.call-update) | async-done | bytes 524304 | tf_op jit(solution)/shard_map/psum | solution.py:163
  94.5 61.0 %while.24 = (s32[]{:T(128)}, f32[8,128,256]{1,2,0:T(8,128)S(1)}, s32[8,256]{1,0:T(8,128)S(1)}, f32[128,2048]{1,0:T(8,128)S(1)}, s32[]{:T(128)}) while((s32[]{:T(128)}, f32[8,128,256]{1,2,0:T(8,128)S(1)}, s32[8,256]{1,0:T(8,128)S(1)}, f32[128,2048]{1,0:T(8,128)S(1)}, s32[]{:T(128)}) %tuple.75), condition=%wide.region_3.4_spmd.clone, body=%wide.region_2.3_spmd.clone.sunk | while | flops 809500672 | bytes 5377093 | solution.py:71
  159.7 6.0 all-to-all-start
  169.8 21.2 %all-to-all-done = f32[8,1,32768]{2,1,0:T(1,128)S(1)} async-done(((f32[8,1,32768]{2,1,0:T(1,128)}), f32[8,1,32768]{2,1,0:T(1,128)S(1)}, u32[]{:S(2)}, u32[]{:S(2)}) %all-to-all-start) | async-done | bytes 1048608 | tf_op jit(solution)/shard_map/all_to_all | solution.py:165
  215.3 23.1 %all-to-all-done.1 = f32[2,512,256]{2,0,1:T(2,128)S(1)} async-done(((f32[2,512,256]{2,0,1:T(2,128)}), f32[2,512,256]{2,0,1:T(2,128)S(1)}, u32[]{:S(2)}, u32[]{:S(2)}) %all-to-all-start.1) | async-done | bytes 1048608 | tf_op jit(solution)/shard_map/all_to_all | solution.py:186
  242.5 322.5 %while.23 = (s32[]{:T(128)}, f32[32,2,4096]{2,1,0:T(2,128)}, s32[32,32]{1,0:T(8,128)}, f32[16,256,128]{2,1,0:T(8,128)S(1)}, f32[32,2,31,256]{3,1,2,0:T(2,128)}, /*index=5*/s32[32,32]{1,0:T(8,128)}, s32[]{:T(128)}) while((s32[]{:T(128)}, f32[32,2,4096]{2,1,0:T(2,128)}, s32[32,32]{1,0:T(8,128)}, f32[16,256,128]{2,1,0:T(8,128)S(1)}, ...), condition=%wide.region_5.6_spmd, body=%wide.region_4.5_spmd.sunk | while | flops 25168064 | bytes 12949077 | solution.py:116
  317.9 5.1 fusion.169
  328.0 5.1 fusion.169
  348.1 5.1 fusion.169
  358.2 5.1 fusion.169
  388.4 5.1 fusion.169
  408.6 5.1 fusion.169
  438.8 5.1 fusion.169
  448.9 5.1 fusion.169
  489.1 5.1 fusion.169
  509.3 5.1 fusion.169
  519.4 5.1 fusion.169
  539.5 5.1 fusion.169
  549.6 5.1 fusion.169
  590.6 6.0 reshape.230
  596.7 31.5 %all_to_all.45 = f32[16,1,16384]{2,1,0:T(1,128)S(1)} all-to-all(f32[16,1,16384]{2,1,0:T(1,128)S(1)} %reshape.230), channel_id=1, replica_groups=mesh['scene'=2,'pulse'=8,'scat'=2] {'pulse','scat'}, dimensions={0} | all-to-all | bytes 2097152 | tf_op jit(solution)/shard_map/all_to_all | solution.py:189
  (307 shorter events, 402.4 us)
Async XLA Ops:
  6.5 85.8 %all-reduce.2.cloned.1.call-start = ((), (), s32[]{:S(2)}) async-start(), calls=%async_computation.3 | async-start | bytes 1048576 | tf_op jit(solution)/shard_map/psum | solution.py:163
  92.3 1.5 copy-start.3
  159.7 31.3 %all-to-all-start = ((f32[8,1,32768]{2,1,0:T(1,128)}), f32[8,1,32768]{2,1,0:T(1,128)S(1)}, u32[]{:S(2)}, u32[]{:S(2)}) async-start(f32[8,1,32768]{2,1,0:T(1,128)} %reshape.228), calls=%async_computation | async-start | bytes 2097152 | tf_op jit(solution)/shard_map/all_to_all | solution.py:165
  169.8 32.4 %copy-start.1 = (f32[512,512]{1,0:T(8,128)}, f32[512,512]{1,0:T(8,128)S(1)}, u32[]{:S(2)}) copy-start(f32[512,512]{1,0:T(8,128)S(1)} %get-tuple-element.214) | copy-start | bytes 3145732
  191.0 1.0 copy-start.4
  210.2 28.2 %all-to-all-start.1 = ((f32[2,512,256]{2,0,1:T(2,128)}), f32[2,512,256]{2,0,1:T(2,128)S(1)}, u32[]{:S(2)}, u32[]{:S(2)}) async-start(f32[2,512,256]{2,0,1:T(2,128)} %copy.55), calls=%async_computation.1 | async-start | bytes 2097152 | tf_op jit(solution)/shard_map/all_to_all | solution.py:186
  239.5 2.9 copy-start
  639.7 1.2 copy-start.2
Sparse Core Ops, SparseCore 0:
  71.2 21.0 all-reduce.1
where the time goes:
time: 666 us; the launch traced here: 653 us
  matrix products  205 us (31%)
  local copies, waits for them, and re-layouts  194 us (29%)
  other arithmetic  131 us (20%)
  waiting for transfers between devices  65.4 us (10%)
  blocking collectives  31.5 us (5%)
  between operations  14.2 us (2%)
  starting transfers between devices  11 us (2%)
    dot_general x32, matrix products, one_row(): jnp.einsum('cbu,but->cbt', chosen, kernels, precision=highest_frequency)  163 us
    gather x32, local copies, waits for them, and re-layouts, one_row(): kernels = kernel_bank[chosen_kinds]  88.8 us
    scatter-add x1, other arithmetic, binning(): return jax.ops.segment_sum(stacked, target, num_segments=B)  45.3 us
    cos x8, other arithmetic, tables(): return (jnp.cos(angle), jnp.sin(angle))  32.7 us
    all_to_all x1, blocking collectives, on_device(): lax.all_to_all(ranged, ('pulse', 'scat'), split_axis=2, concat_axis=1, ti...  31.5 us
    dot_general x8, matrix products, one_block(): jnp.dot(left_matrix, right_matrix, precision=highest_frequency, preferred...  27.9 us
    squeeze x32, local copies, waits for them, and re-layouts, stolt(): lax.map(one_row, (windows.transpose(1, 0, 2, 3), first_blocks, kinds))  27 us
    all_to_all x1, waiting for transfers between devices, on_device(): lax.all_to_all(spectrum, ('pulse', 'scat'), split_axis=1, concat_axis=2,...  23.1 us
  transfers between devices with their start and end apart: 3, of which 3 were waited for; matrix products, arithmetic and copies ran while one was open for 1% of the time, Pallas kernels for 0%

commit v1 on v0

v1 whole, which is shorter than its diff:
```python
import functools

import jax
import jax.numpy as jnp
import numpy as np
from jax import lax
from jax.experimental import pallas as pl
from jax.experimental.pallas import tpu as pltpu
from jax.sharding import PartitionSpec as P

P_SIZE = 512
F_LEN = 4096
B = 1024
SHIFT = 16
STOLT = 128
BLOCKS = 32
SPACING = 2.0
NEAR = 700000.0
BIN_SIDE = 32
GROUP = 4
HIGH = lax.Precision.HIGH
f32 = jnp.float32
bf16 = jnp.bfloat16


def trig_coefs():
    x = np.cos(np.pi * (np.arange(400) + 0.5) / 400) * 0.5
    u = x * x
    s = np.polynomial.chebyshev.Chebyshev.fit(u, np.sin(np.pi * x) / x, 5).convert(
        kind=np.polynomial.Polynomial
    )
    c = np.polynomial.chebyshev.Chebyshev.fit(u, np.cos(np.pi * x), 5).convert(
        kind=np.polynomial.Polynomial
    )
    return [float(v) for v in s.coef], [float(v) for v in c.coef]


def horner(u, coefs):
    acc = jnp.full_like(u, coefs[-1])
    for c in coefs[-2::-1]:
        acc = acc * u + c
    return acc


def split(x):
    hi = x.astype(bf16)
    lo = (x - hi.astype(f32)).astype(bf16)
    return hi, lo


def np_split(x):
    x = np.asarray(x, np.float64)
    hi = np.asarray(x, jnp.bfloat16)
    lo = np.asarray(x - hi.astype(np.float64), jnp.bfloat16)
    return np.stack([hi, lo])


def dots(a, b, dims):
    d = functools.partial(
        lax.dot_general, dimension_numbers=(dims, ((), ())), preferred_element_type=f32
    )
    return d(a[0], b[0]) + (d(a[0], b[1]) + d(a[1], b[0]))


def bin_kernel(pulse_base, pos, amp, tgt, bnc, out, acc, *, pulses, sin_c, cos_c):
    step = pl.program_id(0)
    width = pos.shape[1]

    @pl.when(step == 0)
    def _():
        acc[...] = jnp.zeros_like(acc)

    base = pulse_base[0]
    ids = base + lax.broadcasted_iota(jnp.int32, (pulses, width), 0)
    along = (ids.astype(f32) - P_SIZE // 2) * SPACING
    target = tgt[...]
    slant = NEAR + target.astype(f32)
    offset = along - pos[...]
    square = offset * offset
    excess = square / (jnp.sqrt(slant * slant + square) + slant)
    halves = excess * -128.0
    whole = jnp.round(halves)
    r = halves - whole
    u = r * r
    odd = whole - 2.0 * jnp.floor(whole * 0.5)
    sign = 1.0 - 2.0 * odd
    sin_p = sign * r * horner(u, sin_c)
    cos_p = sign * horner(u, cos_c)
    flip = 1.0 - 2.0 * bnc[...].astype(f32)
    are = flip * amp[0:1]
    aim = flip * amp[1:2]
    re = are * cos_p - aim * sin_p
    im = are * sin_p + aim * cos_p
    steer = jnp.concatenate([re, im], 0)
    hi, lo = split(steer)
    rhs = jnp.concatenate([hi, lo], 0)
    bins = lax.broadcasted_iota(jnp.int32, (B, width), 0)
    hot = jnp.where(bins == target, 1.0, 0.0).astype(bf16)
    acc[...] += lax.dot_general(
        hot, rhs, (((1,), (1,)), ((), ())), preferred_element_type=f32
    )

    @pl.when(step == pl.num_programs(0) - 1)
    def _():
        out[...] = acc[:, : 2 * pulses] + acc[:, 2 * pulses :]


def binning(positions, amplitude, target, bounce, pulse_base, pulses):
    count = positions.shape[0]
    width = min(512, count)
    sin_c, cos_c = trig_coefs()
    row = lambda n: pl.BlockSpec((n, width), lambda i: (0, i))
    return pl.pallas_call(
        functools.partial(bin_kernel, pulses=pulses, sin_c=sin_c, cos_c=cos_c),
        grid=(count // width,),
        in_specs=[pl.BlockSpec(memory_space=pltpu.SMEM), row(1), row(2), row(1), row(1)],
        out_specs=pl.BlockSpec((B, 2 * pulses), lambda i: (0, 0)),
        out_shape=jax.ShapeDtypeStruct((B, 2 * pulses), f32),
        scratch_shapes=[pltpu.VMEM((B, 4 * pulses), f32)],
        name="binning",
    )(
        pulse_base.reshape(1),
        positions.reshape(1, count),
        amplitude,
        target.reshape(1, count),
        bounce.reshape(1, count),
    )


def complex_rows(c, s):
    return np.block([[c, s], [-s, c]])


def mid_tables(n_dev):
    side = np.arange(BIN_SIDE)
    t = np.arange(STOLT)
    eye = np.eye(GROUP)
    a = -2 * np.pi / STOLT * ((side[:, None] * t[None, :]) % STOLT)
    ta = complex_rows(np.cos(a), np.sin(a))
    a = -2 * np.pi / F_LEN * (side[:, None] * t[None, :])
    wa = np.stack([np.tile(np.cos(a), (GROUP, 1)), np.tile(np.sin(a), (GROUP, 1))])
    a = -2 * np.pi / BIN_SIDE * ((side[:, None] * side[None, :]) % BIN_SIDE)
    c, s = np.kron(eye, np.cos(a)), np.kron(eye, np.sin(a))
    tb = complex_rows(c, s).T
    blk = np.arange(BLOCKS)
    a = 2 * np.pi / BLOCKS * ((blk[:, None] * blk[None, :]) % BLOCKS)
    c, s = np.kron(eye, np.cos(a)), np.kron(eye, np.sin(a))
    tc = complex_rows(c, s)
    a = 2 * np.pi / F_LEN * (t[:, None] * blk[None, :])
    wc = np.stack([np.tile(np.cos(a), (1, GROUP)), np.tile(np.sin(a), (1, GROUP))])
    a = 2 * np.pi / STOLT * ((t[:, None] * t[None, :]) % STOLT)
    td = complex_rows(np.cos(a), np.sin(a)).T / F_LEN
    td = td.reshape(2, n_dev, STOLT // n_dev, 2 * STOLT).transpose(1, 0, 2, 3)
    td = td.reshape(2 * STOLT, 2 * STOLT)
    return (
        np_split(ta),
        wa.astype(np.float32),
        np_split(tb),
        np_split(tc),
        wc.astype(np.float32),
        np_split(td),
    )


def mid_kernel(x, phase, hot, kind, bank, ta, wa, tb, tc, wc, td, out, *, subs):
    n = GROUP * BLOCKS
    parts_hi, parts_lo = [], []
    for g in range(subs):
        lanes = slice(g * n, (g + 1) * n)
        y = dots(split(x[:, lanes]), (ta[0], ta[1]), ((0,), (0,)))
        yr, yi = y[:, :STOLT], y[:, STOLT:]
        y = jnp.concatenate([yr * wa[0] - yi * wa[1], yr * wa[1] + yi * wa[0]], 0)
        z = dots((tb[0], tb[1]), split(y), ((1,), (0,)))
        zr, zi = z[:n], z[n:]
        cp, sp = phase[0, lanes], phase[1, lanes]
        z = jnp.concatenate([zr * cp - zi * sp, zr * sp + zi * cp], 1)
        hi, lo = split(z)
        picked = jnp.dot(
            hot[g], jnp.concatenate([hi, lo], 1), preferred_element_type=f32
        ).astype(bf16)
        first, second = picked[:n], picked[n:]
        for c in range(2):
            for base, keep in ((0, parts_hi), (2 * STOLT, parts_lo)):
                cut = slice(base + c * STOLT, base + (c + 1) * STOLT)
                keep.append(jnp.concatenate([first[:, cut], second[:, cut]], 1))
    ghi = jnp.concatenate(parts_hi, 0)
    glo = jnp.concatenate(parts_lo, 0)
    kinds = kind[...].reshape(subs * 2 * n, 1)
    kinds = jnp.broadcast_to(kinds, (subs * 2 * n, STOLT))
    acc = jnp.zeros((subs * 2 * n, STOLT), f32)
    for k in range(bank.shape[1]):
        r = dots((ghi, glo), (bank[0, k], bank[1, k]), ((1,), (0,)))
        for half in range(2):
            acc = jnp.where(kinds == 2 * k + half, r[:, half * STOLT : (half + 1) * STOLT], acc)
    for g in range(subs):
        s = acc[g * 2 * n : (g + 1) * 2 * n]
        y = dots(split(s), (tc[0], tc[1]), ((0,), (0,)))
        yr, yi = y[:, :n], y[:, n:]
        y = jnp.concatenate([yr * wc[0] - yi * wc[1], yr * wc[1] + yi * wc[0]], 0)
        out[:, g * n : (g + 1) * n] = dots((td[0], td[1]), split(y), ((1,), (0,)))


def middle(x, phase, hot, kind, bank, tables):
    rows = x.shape[1] // BIN_SIDE
    groups = rows // GROUP
    subs = min(2, groups)
    n = GROUP * BLOCKS
    whole = lambda a: pl.BlockSpec(a.shape, lambda i: (0,) * a.ndim)
    return pl.pallas_call(
        functools.partial(mid_kernel, subs=subs),
        grid=(groups // subs,),
        in_specs=[
            pl.BlockSpec((x.shape[0], subs * n), lambda i: (0, i)),
            pl.BlockSpec((2, subs * n, STOLT), lambda i: (0, i, 0)),
            pl.BlockSpec((subs, 2 * n, n), lambda i: (i, 0, 0)),
            pl.BlockSpec((subs, 2 * n, 1), lambda i: (i, 0, 0)),
            whole(bank),
        ]
        + [whole(t) for t in tables],
        out_specs=pl.BlockSpec((2 * STOLT, subs * n), lambda i: (0, i)),
        out_shape=jax.ShapeDtypeStruct((2 * STOLT, groups * n), f32),
        name="middle",
    )(x, phase, hot, kind, bank, *tables)


def reference_phase(row_ids, cols):
    centered = (row_ids + P_SIZE // 2) % P_SIZE - P_SIZE // 2
    along_k = 2.0 * jnp.pi / (P_SIZE * SPACING) * centered.astype(f32)
    kr = 4.0 * jnp.pi / 3e8 * (9.6e9 + (cols.astype(f32) - F_LEN // 2) * (1.5e8 / F_LEN))
    squared = along_k * along_k
    depth = NEAR + B // 2
    return (
        -depth
        * squared[:, None]
        / (jnp.sqrt(kr[None, :] * kr[None, :] - squared[:, None]) + kr[None, :])
    )


def on_device(positions, amplitude, range_cells, bounce, stolt_block, kernel_choice, kernel_bank):
    n_pulse = lax.axis_size("pulse")
    n_scat = lax.axis_size("scat")
    n_dev = n_pulse * n_scat
    pulse_here = lax.axis_index("pulse")
    scat_here = lax.axis_index("scat")
    pulses = P_SIZE // n_pulse
    rows = P_SIZE // n_dev
    width = F_LEN // n_dev
    groups = rows // GROUP
    n = GROUP * BLOCKS
    bins_scat = B // n_scat
    bins_here = bins_scat // n_pulse

    ids = jnp.arange(GROUP, dtype=jnp.int32)[None, :, None] * BLOCKS
    first = stolt_block.reshape(groups, GROUP, BLOCKS) + ids
    pick = jnp.stack([first, first + 1], 1).reshape(groups, 2 * n, 1)
    hot = (pick == jnp.arange(n, dtype=jnp.int32)[None, None, :]).astype(bf16)
    kind = jnp.stack([kernel_choice.reshape(groups, n)] * 2, 1).reshape(groups, 2 * n, 1)
    kernels = kernel_bank.shape[0]
    bank = kernel_bank.reshape(kernels // 2, 2, 2 * STOLT, STOLT).transpose(0, 2, 1, 3)
    bank = bank.reshape(kernels // 2, 2 * STOLT, 2 * STOLT)
    bank_hi = lax.reduce_precision(bank, 8, 7)
    bank = jnp.stack([bank_hi.astype(bf16), (bank - bank_hi).astype(bf16)])
    row_ids = (pulse_here * n_scat + scat_here) * rows + jnp.arange(rows, dtype=jnp.int32)
    theta = reference_phase(row_ids, jnp.arange(F_LEN, dtype=jnp.int32))
    theta = theta.reshape(rows * BLOCKS, STOLT)
    phase = jnp.stack([jnp.cos(theta), jnp.sin(theta)])

    target = range_cells + SHIFT * bounce
    partial = binning(positions, amplitude, target, bounce, pulse_here * pulses, pulses)
    partial = partial.reshape(n_scat, bins_scat, 2 * pulses)
    binned = lax.dynamic_index_in_dim(partial, scat_here, 0, keepdims=False)
    for shift in range(1, n_scat):
        other = lax.dynamic_index_in_dim(
            partial, (scat_here + shift) % n_scat, 0, keepdims=False
        )
        ring = [(i, (i + shift) % n_scat) for i in range(n_scat)]
        binned = binned + lax.ppermute(other, "scat", ring)

    turned = lax.all_to_all(
        binned.reshape(n_pulse, bins_here, 2 * pulses), "pulse", 0, 0, tiled=True
    )
    turned = turned.reshape(n_pulse, bins_here, 2, pulses).transpose(0, 3, 2, 1)
    turned = turned.reshape(P_SIZE, 2 * bins_here)
    k = np.arange(P_SIZE)
    angle = 2 * np.pi / P_SIZE * ((k[:, None] * k[None, :]) % P_SIZE)
    az = jnp.asarray(np.concatenate([np.cos(angle), np.sin(angle)], 0), f32)
    product = jnp.dot(az, turned, precision=HIGH, preferred_element_type=f32)
    pc, ps = product[:P_SIZE], product[P_SIZE:]
    spectrum = pc + jnp.concatenate([ps[:, bins_here:], -ps[:, :bins_here]], 1)

    az_rows = lax.all_to_all(
        spectrum.reshape(n_dev, rows, 2 * bins_here), ("pulse", "scat"), 0, 0, tiled=True
    )
    x = az_rows.reshape(n_pulse, n_scat, rows, 2, bins_here).transpose(3, 1, 0, 4, 2)
    x = x.reshape(2, BIN_SIDE, BIN_SIDE, rows).transpose(0, 1, 3, 2)
    x = x.reshape(2 * BIN_SIDE, rows * BIN_SIDE)
    tables = tuple(jnp.asarray(t) for t in mid_tables(n_dev))
    ranged = middle(x, phase, hot, kind, bank, tables)

    per = STOLT // n_dev
    columns = lax.all_to_all(
        ranged.reshape(n_dev, 2 * per, rows * BLOCKS), ("pulse", "scat"), 0, 0, tiled=True
    )
    columns = columns.reshape(n_dev, 2, per, rows, BLOCKS).transpose(0, 3, 1, 2, 4)
    columns = columns.reshape(P_SIZE, 2 * width)
    final = jnp.dot(az, columns, precision=HIGH, preferred_element_type=f32)
    fc, fs = final[:P_SIZE], final[P_SIZE:]
    re = (fc[:, :width] - fs[:, width:]) / P_SIZE
    im = (fc[:, width:] + fs[:, :width]) / P_SIZE
    return jnp.stack([re, im])


def solution(mesh):
    placed = (
        P(("scene", "scat")),
        P(None, ("scene", "scat")),
        P(("scene", "scat")),
        P(("scene", "scat")),
        P(("pulse", "scat"), None),
        P(("pulse", "scat"), None),
        P(),
    )
    return jax.shard_map(
        on_device,
        mesh=mesh,
        in_specs=placed,
        out_specs=P(None, "scene", ("pulse", "scat")),
        check_vma=False,
    )
```

time: 666 us -> 130 us (0.20); the launches traced: 653 us -> 129 us
  matrix products: 205 us -> 3 us
  local copies, waits for them, and re-layouts: 194 us -> 32.7 us
  other arithmetic: 131 us -> 14.1 us
  waiting for transfers between devices: 65.4 us -> 4.5 us
  Pallas kernels: 0 us -> 31.4 us
  between operations: 14.2 us -> 0.18 us
    dot_general x50 -> x2, matrix products: 205 us -> 3 us  [the longest x1 1.83 us: on_device(): final = jnp.dot(az, columns, precision=HIGH, preferred_element_type=f32)]
    gather x64 -> x0, local copies, waits for them, and re-layouts: 109 us -> none  [the longest x32 88.8 us: one_row(): kernels = kernel_bank[chosen_kinds]]
    scatter-add x1 -> x0, other arithmetic: 45.3 us -> none  [binning(): return jax.ops.segment_sum(stacked, target, num_segments=B)]
    all_to_all x2, waiting for transfers between devices: 44.3 us -> 4.5 us  [the longest x1 4.5 us: on_device(): lax.all_to_all(spectrum.reshape(n_dev, rows, 2 * bins_here), ('pulse', 's...]
    pallas_call x0 -> x2, Pallas kernels: none -> 31.4 us  [the longest x1 18.3 us: middle(): pl.pallas_call(functools.partial(mid_kernel, subs=subs), grid=(groups //...]
    cos x8 -> x1, other arithmetic: 32.7 us -> 3.57 us  [on_device(): phase = jnp.stack([jnp.cos(theta), jnp.sin(theta)])]
    squeeze x32 -> x1, local copies, waits for them, and re-layouts: 27 us -> 1.04 us  [on_device(): lax.dynamic_index_in_dim(partial, (scat_here + shift) % n_scat, 0, keepdi...]
    select_n x32 -> x0, other arithmetic: 22.8 us -> none  [one_row(): kernels = kernel_bank[chosen_kinds]]
  transfers between devices with their start and end apart: 3 -> 3, of which waited for: 3 -> 1; matrix products, arithmetic and copies ran while one was open for 1% -> 14% of each run, Pallas kernels for 0% -> 0%
where the time goes in v1:
time: 130 us; the launch traced here: 129 us
  local copies, waits for them, and re-layouts  32.7 us (25%)
  Pallas kernels  31.4 us (24%)
  blocking collectives  29.3 us (23%)
  other arithmetic  14.1 us (11%)
  starting transfers between devices  13.4 us (10%)
  waiting for transfers between devices  4.5 us (3%)
  matrix products  3 us (2%)
    all_to_all x1, blocking collectives, on_device(): lax.all_to_all(ranged.reshape(n_dev, 2 * per, rows * BLOCKS), ('pulse', '...  29.3 us
    pallas_call x1, Pallas kernels, middle(): pl.pallas_call(functools.partial(mid_kernel, subs=subs), grid=(groups //...  18.3 us
    pallas_call x1, Pallas kernels, binning(): pl.pallas_call(functools.partial(bin_kernel, pulses=pulses, sin_c=sin_c,...  13 us
    transpose x1, local copies, waits for them, and re-layouts, on_device(): columns.reshape(n_dev, 2, per, rows, BLOCKS).transpose(0, 3, 1, 2, 4)  7.4 us
    all_to_all x1, starting transfers between devices, on_device(): lax.all_to_all(binned.reshape(n_pulse, bins_here, 2 * pulses), 'pulse', 0...  6.99 us
    all_to_all x1, starting transfers between devices, on_device(): lax.all_to_all(spectrum.reshape(n_dev, rows, 2 * bins_here), ('pulse', 's...  6.32 us
    all_to_all x1, waiting for transfers between devices, on_device(): lax.all_to_all(spectrum.reshape(n_dev, rows, 2 * bins_here), ('pulse', 's...  4.5 us
    cos x1, other arithmetic, on_device(): phase = jnp.stack([jnp.cos(theta), jnp.sin(theta)])  3.57 us
  transfers between devices with their start and end apart: 3, of which 1 were waited for; matrix products, arithmetic and copies ran while one was open for 14% of the time, Pallas kernels for 0%

profile of v1, /device:TPU:1, one launch (start us, length us, event | category | flops | bytes accessed | tf_op | source)
XLA Modules:
  0.0 128.6 jit_solution(15394957971999473905)
XLA Ops:
  0.0 1.4 %multiply_add_fusion = s32[8192]{0:T(1024)} fusion(s32[8192]{0:T(1024)} %param.16, s32[8192]{0:T(1024)} %param.17), kind=kLoop, calls=%fused_computation.27 | loop fusion | flops 16384 | bytes 98304 | tf_op jit(solution)/shard_map/add | solution.py:268
  1.4 13.0 %binning.1 = f32[1024,128]{1,0:T(8,128)} custom-call(s32[1]{0:T(128)} %bitcast.pulse_base, f32[1,8192]{1,0:T(1,128)} %bitcast.79, f32[2,8192]{1,0:T(2,128)} %amp.1, s32[1,8192]{1,0:T(1,128)} %bitcast.78, s32[1,8192]{1,0:T(1,128)} %bitcast.77), custom_call_target="tpu_custom_call" | custom-call | tf_op jit(solution)/shard_map/binning/pallas_call | solution.py:113
  16.9 3.6 %fusion.9 = (f32[1,1024,128]{2,1,0:T(8,128)}, f32[1,1024,128]{2,1,0:T(8,128)}) fusion(f32[1024]{0:T(1024)S(1)} %sub.58, f32[1024]{0:T(1024)S(1)} %div.31, f32[1,1024,128]{2,1,0:T(8,128)S(1)} %bitcast.74, f32[1,1024,128]{2,1,0:T(8,128)S(1)} %bitcast.75), kind=kLoop, calls=%fused_computation.21 | loop fusion | flops 393216 | bytes 2105344 | tf_op jit(solution)/shard_map/cos | solution.py:266
  21.2 7.0 %all-to-all-start = ((f32[8,64,128]{2,1,0:T(8,128)}), f32[8,64,128]{2,1,0:T(8,128)S(1)}, u32[]{:S(2)}, u32[]{:S(2)}) async-start(f32[8,64,128]{2,1,0:T(8,128)} %bitcast.7), calls=%async_computation | async-start | bytes 524288 | tf_op jit(solution)/shard_map/all_to_all | solution.py:279
  28.3 1.4 %copy.31.kind = s32[8,256,1]{2,1,0:T(8,128)} copy(s32[8,256,1]{1,0,2:T(8,128)S(1)} %add_bitcast_fusion) | data formatting | bytes 16384 | tf_op jit(solution)/shard_map/reshape | solution.py:257
  29.7 3.0 %copy.35 = f32[8,2,256,128]{3,1,2,0:T(2,128)} copy(f32[8,2,256,128]{3,2,1,0:T(8,128)S(1)} %bitcast.70) | data formatting | bytes 4194304 | tf_op jit(solution)/shard_map/reshape | solution.py:259
  32.7 2.9 %reshape.322 = f32[1,8,256,256]{3,2,1,0:T(8,128)S(1)} reshape(f32[8,256,2,128]{3,2,1,0:T(2,128)} %bitcast.66) | data formatting | bytes 4194304 | tf_op jit(solution)/shard_map/reshape | solution.py:260
  35.6 1.4 %reduce-precision_convert_fusion = (bf16[1,8,256,256]{3,2,1,0:T(8,128)(2,1)S(1)}, bf16[1,8,256,256]{3,2,1,0:T(8,128)(2,1)}) fusion(f32[1,8,256,256]{3,2,1,0:T(8,128)S(1)} %reshape.322), kind=kLoop, calls=%fused_computation.1 | loop fusion | flops 2097152 | bytes 4194304 | tf_op jit(solution)/shard_map/convert_element_type | solution.py:262
  38.1 2.1 %copy.25 = f32[8,64,2,64]{1,0,3,2:T(8,128)} copy(f32[8,64,2,64]{1,2,3,0:T(2,128)} %bitcast.73) | data formatting | bytes 524288 | tf_op jit(solution)/shard_map/transpose | solution.py:282
  40.2 1.2 reshape.314
  41.4 1.2 fusion.17
  43.5 6.3 %all-to-all-start.1 = ((f32[16,32,128]{2,1,0:T(8,128)}), f32[16,32,128]{2,1,0:T(8,128)S(1)}, u32[]{:S(2)}, u32[]{:S(2)}) async-start(f32[16,32,128]{2,1,0:T(8,128)} %bitcast.76), calls=%async_computation.1 | async-start | bytes 524288 | tf_op jit(solution)/shard_map/all_to_all | solution.py:291
  49.9 2.4 %pad_maximum_fusion.1.phase = f32[2,1024,128]{2,1,0:T(8,128)} fusion(f32[1,1024,128]{2,1,0:T(8,128)} %get-tuple-element.12, f32[1,1024,128]{2,1,0:T(8,128)} %get-tuple-element.11), kind=kLoop, calls=%fused_computation.5 | loop fusion | flops 262144 | bytes 2097152 | tf_op jit(solution)/shard_map/stack | solution.py:266
  52.2 1.5 %pad_maximum_fusion.bank = bf16[2,8,256,256]{3,2,1,0:T(8,128)(2,1)} fusion(bf16[1,8,256,256]{3,2,1,0:T(8,128)(2,1)S(1)} %copy-done.1, bf16[1,8,256,256]{3,2,1,0:T(8,128)(2,1)S(1)} %get-tuple-element.9), kind=kLoop, calls=%fused_computation.3 | loop fusion | flops 1048576 | bytes 4194304 | tf_op jit(solution)/shard_map/stack | solution.py:262
  54.9 4.5 %all-to-all-done.1 = f32[16,32,128]{2,1,0:T(8,128)S(1)} async-done(((f32[16,32,128]{2,1,0:T(8,128)}), f32[16,32,128]{2,1,0:T(8,128)S(1)}, u32[]{:S(2)}, u32[]{:S(2)}) %all-to-all-start.1) | async-done | bytes 262176 | tf_op jit(solution)/shard_map/all_to_all | solution.py:291
  60.0 1.2 reshape.317
  61.2 1.8 %copy.28 = f32[2,32,32,32]{3,2,1,0:T(8,128)S(1)} copy(f32[2,32,32,32]{3,1,2,0:T(8,128)} %bitcast.68) | data formatting | bytes 524288 | tf_op jit(solution)/shard_map/transpose | solution.py:295
  63.0 1.2 reshape.318.x
  64.3 18.3 %middle.1 = f32[256,1024]{1,0:T(8,128)} custom-call(f32[64,1024]{1,0:T(8,128)} %reshape.318.x, f32[2,1024,128]{2,1,0:T(8,128)} %pad_maximum_fusion.1.phase, bf16[8,256,128]{2,1,0:T(8,128)(2,1)} %fusion.1.hot, s32[8,256,1]{2,1,0:T(8,128)} %copy.31.kind, bf16[2,8,256,256]{3,2,1,0:T(8,128)(2,1)} %pad_maximum_fusion.bank, ...), custom_call_target="tpu_custom_call" | custom-call | tf_op jit(solution)/shard_map/middle/pallas_call | solution.py:209
  82.6 29.3 %all_to_all.15 = f32[16,16,1024]{2,1,0:T(8,128)S(1)} all-to-all(f32[16,16,1024]{2,1,0:T(8,128)} %bitcast.67), channel_id=1, replica_groups=mesh['scene'=2,'pulse'=8,'scat'=2] {'pulse','scat'}, dimensions={0} | all-to-all | bytes 2097152 | tf_op jit(solution)/shard_map/all_to_all | solution.py:301
  111.9 2.7 %reshape.324 = f32[16,2,8,32,32]{4,3,2,1,0:T(8,128)} reshape(f32[16,16,1024]{2,1,0:T(8,128)S(1)} %all_to_all.15) | data formatting | bytes 2097152 | tf_op jit(solution)/shard_map/reshape | solution.py:304
  114.6 7.4 %copy.32 = f32[16,32,2,8,32]{4,3,2,1,0:T(8,128)} copy(f32[16,32,2,8,32]{4,1,3,2,0:T(8,128)} %bitcast.65) | data formatting | bytes 2097152 | tf_op jit(solution)/shard_map/transpose | solution.py:304
  122.0 3.5 %reshape.325 = f32[512,512]{1,0:T(8,128)S(1)} reshape(f32[16,32,2,8,32]{4,3,2,1,0:T(8,128)} %copy.32) | data formatting | bytes 2097152 | tf_op jit(solution)/shard_map/reshape | solution.py:305
  125.6 1.8 %fusion.18 = f32[1024,512]{1,0:T(8,128)S(1)} fusion(f32[1024,512]{1,0:T(8,128)S(1)} %copy-done, f32[512,512]{1,0:T(8,128)S(1)} %reshape.325), kind=kOutput, calls=%fused_computation.45 | convolution fusion | flops 1610612736 | bytes 5242880 | tf_op jit(solution)/shard_map/dot_general | solution.py:306
  (40 shorter events, 8.3 us)
Async XLA Ops:
  14.4 6.0 %copy-start.3 = (f32[1024,128]{1,0:T(8,128)S(1)}, f32[1024,128]{1,0:T(8,128)}, u32[]{:S(2)}) copy-start(f32[1024,128]{1,0:T(8,128)} %binning.1) | copy-start | bytes 1572868
  15.5 5.0 %collective-permute-start = (f32[512,128]{1,0:T(8,128)S(1)}, f32[512,128]{1,0:T(8,128)S(1)}, u32[]{:S(2)}, u32[]{:S(2)}) collective-permute-start(f32[512,128]{1,0:T(8,128)S(1)} %dynamic-slice_bitcast_fusion), channel_id=1, source_target_pairs={{0,1},{1,0},{2,3},{3,2},{4,5},{5,4},{6,7},{7,6},{8,9},{9,8},{10,11... | collective-permute-start | bytes 786440 | tf_op jit(solution)/shard_map/ppermute | solution.py:277
  16.8 11.4 %copy-start.4 = (s32[32,32]{1,0:T(8,128)S(1)}, s32[32,32]{1,0:T(8,128)}, u32[]{:S(2)}) copy-start(s32[32,32]{1,0:T(8,128)} %param.19) | copy-start | bytes 12292
  16.8 12.9 %copy-start.2 = (f32[16,256,128]{2,1,0:T(8,128)S(1)}, f32[16,256,128]{2,1,0:T(8,128)}, u32[]{:S(2)}) copy-start(f32[16,256,128]{2,1,0:T(8,128)} %param.20) | copy-start | bytes 6291460
  21.2 15.8 %all-to-all-start = ((f32[8,64,128]{2,1,0:T(8,128)}), f32[8,64,128]{2,1,0:T(8,128)S(1)}, u32[]{:S(2)}, u32[]{:S(2)}) async-start(f32[8,64,128]{2,1,0:T(8,128)} %bitcast.7), calls=%async_computation | async-start | bytes 524288 | tf_op jit(solution)/shard_map/all_to_all | solution.py:279
  36.9 4.5 %copy-start = (f32[1024,512]{1,0:T(8,128)S(1)}, f32[1024,512]{1,0:T(8,128)}, u32[]{:S(2)}) copy-start(f32[1024,512]{1,0:T(8,128)} %constant.86.clone) | copy-start | bytes 6291460
  43.5 15.8 %all-to-all-start.1 = ((f32[16,32,128]{2,1,0:T(8,128)}), f32[16,32,128]{2,1,0:T(8,128)S(1)}, u32[]{:S(2)}, u32[]{:S(2)}) async-start(f32[16,32,128]{2,1,0:T(8,128)} %bitcast.76), calls=%async_computation.1 | async-start | bytes 524288 | tf_op jit(solution)/shard_map/all_to_all | solution.py:291
  49.9 2.4 %copy-start.1 = (bf16[1,8,256,256]{3,2,1,0:T(8,128)(2,1)S(1)}, bf16[1,8,256,256]{3,2,1,0:T(8,128)(2,1)}, u32[]{:S(2)}) copy-start(bf16[1,8,256,256]{3,2,1,0:T(8,128)(2,1)} %get-tuple-element.10) | copy-start | bytes 3145732

commit v2 on v1

--- a/solution.py
+++ b/solution.py
@@ -131,12 +131,12 @@
     return np.block([[c, s], [-s, c]])
 
 
-def mid_tables(n_dev):
+def mid_tables(n_dev, order):
     side = np.arange(BIN_SIDE)
     t = np.arange(STOLT)
     eye = np.eye(GROUP)
     a = -2 * np.pi / STOLT * ((side[:, None] * t[None, :]) % STOLT)
-    ta = complex_rows(np.cos(a), np.sin(a))
+    ta = complex_rows(np.cos(a), np.sin(a))[order]
     a = -2 * np.pi / F_LEN * (side[:, None] * t[None, :])
     wa = np.stack([np.tile(np.cos(a), (GROUP, 1)), np.tile(np.sin(a), (GROUP, 1))])
     a = -2 * np.pi / BIN_SIDE * ((side[:, None] * side[None, :]) % BIN_SIDE)
@@ -162,17 +162,27 @@
     )
 
 
-def mid_kernel(x, phase, hot, kind, bank, ta, wa, tb, tc, wc, td, out, *, subs):
+def mid_kernel(
+    x, cos_p, sin_p, hot, kind, bank_hi, bank_lo, ta, wa, tb, tc, wc, td, out, xs, os, *, subs
+):
     n = GROUP * BLOCKS
+    step = pl.program_id(0)
+    groups = x.shape[1]
+
+    @pl.when(step == 0)
+    def _():
+        for g in range(groups):
+            xs[g] = x[:, g, :]
+
     parts_hi, parts_lo = [], []
     for g in range(subs):
         lanes = slice(g * n, (g + 1) * n)
-        y = dots(split(x[:, lanes]), (ta[0], ta[1]), ((0,), (0,)))
+        y = dots(split(xs[step * subs + g]), (ta[0], ta[1]), ((0,), (0,)))
         yr, yi = y[:, :STOLT], y[:, STOLT:]
         y = jnp.concatenate([yr * wa[0] - yi * wa[1], yr * wa[1] + yi * wa[0]], 0)
         z = dots((tb[0], tb[1]), split(y), ((1,), (0,)))
         zr, zi = z[:n], z[n:]
-        cp, sp = phase[0, lanes], phase[1, lanes]
+        cp, sp = cos_p[lanes], sin_p[lanes]
         z = jnp.concatenate([zr * cp - zi * sp, zr * sp + zi * cp], 1)
         hi, lo = split(z)
         picked = jnp.dot(
@@ -188,21 +198,27 @@
     kinds = kind[...].reshape(subs * 2 * n, 1)
     kinds = jnp.broadcast_to(kinds, (subs * 2 * n, STOLT))
     acc = jnp.zeros((subs * 2 * n, STOLT), f32)
-    for k in range(bank.shape[1]):
-        r = dots((ghi, glo), (bank[0, k], bank[1, k]), ((1,), (0,)))
+    for k in range(0, bank_hi.shape[0], 2):
+        khi = jnp.concatenate([bank_hi[k], bank_hi[k + 1]], 1)
+        klo = jnp.concatenate([bank_lo[k], bank_lo[k + 1]], 1)
+        r = dots((ghi, glo), (khi, klo), ((1,), (0,)))
         for half in range(2):
-            acc = jnp.where(kinds == 2 * k + half, r[:, half * STOLT : (half + 1) * STOLT], acc)
+            acc = jnp.where(kinds == k + half, r[:, half * STOLT : (half + 1) * STOLT], acc)
     for g in range(subs):
         s = acc[g * 2 * n : (g + 1) * 2 * n]
         y = dots(split(s), (tc[0], tc[1]), ((0,), (0,)))
         yr, yi = y[:, :n], y[:, n:]
         y = jnp.concatenate([yr * wc[0] - yi * wc[1], yr * wc[1] + yi * wc[0]], 0)
-        out[:, g * n : (g + 1) * n] = dots((td[0], td[1]), split(y), ((1,), (0,)))
-
-
-def middle(x, phase, hot, kind, bank, tables):
-    rows = x.shape[1] // BIN_SIDE
-    groups = rows // GROUP
+        os[step * subs + g] = dots((td[0], td[1]), split(y), ((1,), (0,)))
+
+    @pl.when(step == pl.num_programs(0) - 1)
+    def _():
+        for g in range(groups):
+            out[:, g, :] = os[g]
+
+
+def middle(x, cos_p, sin_p, hot, kind, bank_hi, bank_lo, tables):
+    groups = x.shape[1]
     subs = min(2, groups)
     n = GROUP * BLOCKS
     whole = lambda a: pl.BlockSpec(a.shape, lambda i: (0,) * a.ndim)
@@ -210,17 +226,110 @@
         functools.partial(mid_kernel, subs=subs),
         grid=(groups // subs,),
         in_specs=[
-            pl.BlockSpec((x.shape[0], subs * n), lambda i: (0, i)),
-            pl.BlockSpec((2, subs * n, STOLT), lambda i: (0, i, 0)),
+            whole(x),
+            pl.BlockSpec((subs * n, STOLT), lambda i: (i, 0)),
+            pl.BlockSpec((subs * n, STOLT), lambda i: (i, 0)),
             pl.BlockSpec((subs, 2 * n, n), lambda i: (i, 0, 0)),
             pl.BlockSpec((subs, 2 * n, 1), lambda i: (i, 0, 0)),
-            whole(bank),
+            whole(bank_hi),
+            whole(bank_lo),
         ]
         + [whole(t) for t in tables],
-        out_specs=pl.BlockSpec((2 * STOLT, subs * n), lambda i: (0, i)),
-        out_shape=jax.ShapeDtypeStruct((2 * STOLT, groups * n), f32),
+        out_specs=pl.BlockSpec((2 * STOLT, groups, n), lambda i: (0, 0, 0)),
+        out_shape=jax.ShapeDtypeStruct((2 * STOLT, groups, n), f32),
+        scratch_shapes=[
+            pltpu.VMEM((groups, x.shape[0], n), f32),
+            pltpu.VMEM((groups, 2 * STOLT, n), f32),
+        ],
         name="middle",
-    )(x, phase, hot, kind, bank, *tables)
+    )(x, cos_p, sin_p, hot, kind, bank_hi, bank_lo, *tables)
+
+
+def quarter_tables():
+    q = P_SIZE // 4
+    m = np.arange(q)
+    fwd, inv = [], []
+    for low in range(4):
+        a = 2 * np.pi / P_SIZE * (((4 * m[:, None] + low) * m[None, :]) % P_SIZE)
+        fwd.append(np.concatenate([np.cos(a), np.sin(a)], 0))
+        inv.append(np.concatenate([np.cos(a.T), np.sin(a.T)], 0) / P_SIZE)
+    return np_split(np.stack(fwd)), np_split(np.stack(inv))
+
+
+def swap_blocks(arrays):
+    count = len(arrays)
+    lanes = arrays[0].shape[-1]
+    size = lanes // count
+    block = lax.broadcasted_iota(jnp.int32, arrays[0].shape, 1) // size
+    outs = []
+    for b in range(count):
+        acc = None
+        for a in range(count):
+            shift = (a - b) % count * size
+            moved = pltpu.roll(arrays[a], shift, 1) if shift else arrays[a]
+            acc = moved if acc is None else jnp.where(block == a, moved, acc)
+        outs.append(acc)
+    return outs
+
+
+def azimuth_kernel(x, table, out):
+    srcs, bins, lanes = x.shape
+    half = lanes // 2
+    low = lax.broadcasted_iota(jnp.int32, (bins, lanes), 1) < half
+    quarters = []
+    for q in range(4):
+        a, b = x[2 * q], x[2 * q + 1]
+        re = jnp.where(low, a, pltpu.roll(b, half, 1))
+        im = jnp.where(low, pltpu.roll(a, half, 1), b)
+        quarters.append((re, im))
+    (r0, i0), (r1, i1), (r2, i2), (r3, i3) = quarters
+    sr, si, dr, di = r0 + r2, i0 + i2, r0 - r2, i0 - i2
+    tr, ti, er, ei = r1 + r3, i1 + i3, r1 - r3, i1 - i3
+    mixed = (
+        (sr + tr, si + ti),
+        (dr + ei, di - er),
+        (sr - tr, si - ti),
+        (dr - ei, di + er),
+    )
+    size = P_SIZE // 4
+    low = lax.broadcasted_iota(jnp.int32, (size, lanes), 1) < half
+    rows = []
+    for k in range(4):
+        u = jnp.concatenate(mixed[k], 0)
+        g = dots((table[0, k], table[1, k]), split(u), ((1,), (1,)))
+        turned = pltpu.roll(g[size:], half, 1)
+        rows.append(g[:size] + jnp.where(low, turned, -turned))
+    for q, z in enumerate(swap_blocks(rows)):
+        out[:, q] = z.reshape(out.shape[0], out.shape[2], lanes)
+
+
+def image_kernel(x, table, out):
+    devs, _, per, kh, lanes = x.shape
+    size = P_SIZE // 4
+    columns = [[] for _ in range(4)]
+    for c in range(2):
+        for h in range(per // 4):
+            tiles = [x[:, c, 4 * h + j].reshape(devs * kh, lanes) for j in range(4)]
+            for k, z in enumerate(swap_blocks(tiles)):
+                columns[k].append(z)
+    width = lanes * (per // 4)
+    v = []
+    for k in range(4):
+        g = dots((table[0, k], table[1, k]), split(jnp.concatenate(columns[k], 1)), ((1,), (0,)))
+        cos_g, sin_g = g[:size], g[size:]
+        v.append((cos_g[:, :width] - sin_g[:, width:], cos_g[:, width:] + sin_g[:, :width]))
+    (r0, i0), (r1, i1), (r2, i2), (r3, i3) = v
+    sr, si, dr, di = r0 + r2, i0 + i2, r0 - r2, i0 - i2
+    tr, ti, er, ei = r1 + r3, i1 + i3, r1 - r3, i1 - i3
+    mixed = (
+        (sr + tr, si + ti),
+        (dr - ei, di + er),
+        (sr - tr, si - ti),
+        (dr + ei, di - er),
+    )
+    for q in range(4):
+        for c in range(2):
+            out[c, q * size : (q + 1) * size, :] = mixed[q][c]
 
 
 def reference_phase(row_ids, cols):
@@ -255,15 +364,13 @@
     pick = jnp.stack([first, first + 1], 1).reshape(groups, 2 * n, 1)
     hot = (pick == jnp.arange(n, dtype=jnp.int32)[None, None, :]).astype(bf16)
     kind = jnp.stack([kernel_choice.reshape(groups, n)] * 2, 1).reshape(groups, 2 * n, 1)
-    kernels = kernel_bank.shape[0]
-    bank = kernel_bank.reshape(kernels // 2, 2, 2 * STOLT, STOLT).transpose(0, 2, 1, 3)
-    bank = bank.reshape(kernels // 2, 2 * STOLT, 2 * STOLT)
-    bank_hi = lax.reduce_precision(bank, 8, 7)
-    bank = jnp.stack([bank_hi.astype(bf16), (bank - bank_hi).astype(bf16)])
+    bank_hi = lax.reduce_precision(kernel_bank, 8, 7)
+    bank_lo = (kernel_bank - bank_hi).astype(bf16)
+    bank_hi = bank_hi.astype(bf16)
     row_ids = (pulse_here * n_scat + scat_here) * rows + jnp.arange(rows, dtype=jnp.int32)
     theta = reference_phase(row_ids, jnp.arange(F_LEN, dtype=jnp.int32))
     theta = theta.reshape(rows * BLOCKS, STOLT)
-    phase = jnp.stack([jnp.cos(theta), jnp.sin(theta)])
+    cos_p, sin_p = jnp.cos(theta), jnp.sin(theta)
 
     target = range_cells + SHIFT * bounce
     partial = binning(positions, amplitude, target, bounce, pulse_here * pulses, pulses)
@@ -279,25 +386,50 @@
     turned = lax.all_to_all(
         binned.reshape(n_pulse, bins_here, 2 * pulses), "pulse", 0, 0, tiled=True
     )
-    turned = turned.reshape(n_pulse, bins_here, 2, pulses).transpose(0, 3, 2, 1)
-    turned = turned.reshape(P_SIZE, 2 * bins_here)
-    k = np.arange(P_SIZE)
-    angle = 2 * np.pi / P_SIZE * ((k[:, None] * k[None, :]) % P_SIZE)
-    az = jnp.asarray(np.concatenate([np.cos(angle), np.sin(angle)], 0), f32)
-    product = jnp.dot(az, turned, precision=HIGH, preferred_element_type=f32)
-    pc, ps = product[:P_SIZE], product[P_SIZE:]
-    spectrum = pc + jnp.concatenate([ps[:, bins_here:], -ps[:, :bins_here]], 1)
-
-    az_rows = lax.all_to_all(
-        spectrum.reshape(n_dev, rows, 2 * bins_here), ("pulse", "scat"), 0, 0, tiled=True
-    )
-    x = az_rows.reshape(n_pulse, n_scat, rows, 2, bins_here).transpose(3, 1, 0, 4, 2)
-    x = x.reshape(2, BIN_SIDE, BIN_SIDE, rows).transpose(0, 1, 3, 2)
-    x = x.reshape(2 * BIN_SIDE, rows * BIN_SIDE)
-    tables = tuple(jnp.asarray(t) for t in mid_tables(n_dev))
-    ranged = middle(x, phase, hot, kind, bank, tables)
-
     per = STOLT // n_dev
+    packed = 2 * pulses == 128 and 2 * bins_here == 128 and per % 4 == 0 and groups % 8 == 0
+    if packed:
+        forward, backward = (jnp.asarray(t) for t in quarter_tables())
+        spectrum = pl.pallas_call(
+            azimuth_kernel,
+            out_shape=jax.ShapeDtypeStruct((n_dev, 4, groups, n), f32),
+            name="azimuth",
+        )(turned, forward)
+        x = lax.all_to_all(spectrum, ("pulse", "scat"), 0, 0, tiled=True)
+        x = x.reshape(4 * n_dev, groups, n)
+        local = bins_here // BIN_SIDE
+        i, s, c, l = np.meshgrid(
+            np.arange(n_pulse), np.arange(n_scat), np.arange(2), np.arange(local), indexing="ij"
+        )
+        order = (c * BIN_SIDE + s * (BIN_SIDE // n_scat) + i * local + l).reshape(-1)
+    else:
+        turned = turned.reshape(n_pulse, bins_here, 2, pulses).transpose(0, 3, 2, 1)
+        turned = turned.reshape(P_SIZE, 2 * bins_here)
+        k = np.arange(P_SIZE)
+        angle = 2 * np.pi / P_SIZE * ((k[:, None] * k[None, :]) % P_SIZE)
+        az = jnp.asarray(np.concatenate([np.cos(angle), np.sin(angle)], 0), f32)
+        product = jnp.dot(az, turned, precision=HIGH, preferred_element_type=f32)
+        pc, ps = product[:P_SIZE], product[P_SIZE:]
+        spectrum = pc + jnp.concatenate([ps[:, bins_here:], -ps[:, :bins_here]], 1)
+        az_rows = lax.all_to_all(
+            spectrum.reshape(n_dev, rows, 2 * bins_here), ("pulse", "scat"), 0, 0, tiled=True
+        )
+        x = az_rows.reshape(n_pulse, n_scat, rows, 2, bins_here).transpose(3, 1, 0, 4, 2)
+        x = x.reshape(2, BIN_SIDE, BIN_SIDE, rows).transpose(0, 1, 3, 2)
+        x = x.reshape(2 * BIN_SIDE, groups, n)
+        order = np.arange(2 * BIN_SIDE)
+
+    tables = tuple(jnp.asarray(t) for t in mid_tables(n_dev, order))
+    ranged = middle(x, cos_p, sin_p, hot, kind, bank_hi, bank_lo, tables)
+    if packed:
+        columns = lax.all_to_all(
+            ranged.reshape(n_dev, 2, per, groups, n), ("pulse", "scat"), 0, 0, tiled=True
+        )
+        return pl.pallas_call(
+            image_kernel,
+            out_shape=jax.ShapeDtypeStruct((2, P_SIZE, width), f32),
+            name="image",
+        )(columns, backward)
     columns = lax.all_to_all(
         ranged.reshape(n_dev, 2 * per, rows * BLOCKS), ("pulse", "scat"), 0, 0, tiled=True
     )

time: 130 us -> 107 us (0.82)
  local copies, waits for them, and re-layouts: 32.7 us -> 4.9 us
  Pallas kernels: 31.4 us -> 38.8 us
  waiting for transfers between devices: 4.5 us -> 9.51 us
  other arithmetic: 14.1 us -> 9.75 us
  matrix products: 3 us -> 0 us
    reshape x10 -> x0, local copies, waits for them, and re-layouts: 17.5 us -> none  [the longest x1 3.54 us: on_device(): columns = columns.reshape(P_SIZE, 2 * width)]
    transpose x3 -> x0, local copies, waits for them, and re-layouts: 11.4 us -> none  [the longest x1 7.4 us: on_device(): columns.reshape(n_dev, 2, per, rows, BLOCKS).transpose(0, 3, 1, 2, 4)]
    pallas_call x0 -> x2, Pallas kernels: none -> 6.33 us  [the longest x1 3.74 us: on_device(): pl.pallas_call(image_kernel, out_shape=jax.ShapeDtypeStruct((2, P_SIZE, w...]
    another operation x4 -> x0, other arithmetic: 5.05 us -> none  [the longest x1 2.36 us: on_device(): phase = jnp.stack([jnp.cos(theta), jnp.sin(theta)])]
    sin x0 -> x1, other arithmetic: none -> 3.58 us  [on_device(): cos_p, sin_p = (jnp.cos(theta), jnp.sin(theta))]
    cos x1 -> x0, other arithmetic: 3.57 us -> none  [on_device(): phase = jnp.stack([jnp.cos(theta), jnp.sin(theta)])]
    dot_general x2 -> x0, matrix products: 3 us -> none  [the longest x1 1.83 us: on_device(): final = jnp.dot(az, columns, precision=HIGH, preferred_element_type=f32)]
    all_to_all x1, waiting for transfers between devices: 0.01 us -> 2.56 us  [on_device(): lax.all_to_all(binned.reshape(n_pulse, bins_here, 2 * pulses), 'pulse', 0...]
  transfers between devices with their start and end apart: 3 -> 3, of which waited for: 1 -> 3; matrix products, arithmetic and copies ran while one was open for 14% -> 9% of each run, Pallas kernels for 0% -> 0%
where the time goes in v2:
time: 107 us; the launch traced here: 106 us
  Pallas kernels  38.8 us (36%)
  blocking collectives  30.1 us (28%)
  starting transfers between devices  12.5 us (12%)
  other arithmetic  9.75 us (9%)
  waiting for transfers between devices  9.51 us (9%)
  local copies, waits for them, and re-layouts  4.9 us (5%)
    all_to_all x1, blocking collectives, on_device(): lax.all_to_all(ranged.reshape(n_dev, 2, per, groups, n), ('pulse', 'scat'...  30.1 us
    pallas_call x1, Pallas kernels, middle(): pl.pallas_call(functools.partial(mid_kernel, subs=subs), grid=(groups //...  19.4 us
    pallas_call x1, Pallas kernels, binning(): pl.pallas_call(functools.partial(bin_kernel, pulses=pulses, sin_c=sin_c,...  13 us
    all_to_all x1, starting transfers between devices, on_device(): lax.all_to_all(binned.reshape(n_pulse, bins_here, 2 * pulses), 'pulse', 0...  6.65 us
    all_to_all x1, waiting for transfers between devices, on_device(): x = lax.all_to_all(spectrum, ('pulse', 'scat'), 0, 0, tiled=True)  6.53 us
    all_to_all x1, starting transfers between devices, on_device(): x = lax.all_to_all(spectrum, ('pulse', 'scat'), 0, 0, tiled=True)  5.75 us
    pallas_call x1, Pallas kernels, on_device(): pl.pallas_call(image_kernel, out_shape=jax.ShapeDtypeStruct((2, P_SIZE, w...  3.74 us
    sin x1, other arithmetic, on_device(): cos_p, sin_p = (jnp.cos(theta), jnp.sin(theta))  3.58 us
  transfers between devices with their start and end apart: 3, of which 3 were waited for; matrix products, arithmetic and copies ran while one was open for 9% of the time, Pallas kernels for 0%

profile of v2, /device:TPU:1, one launch (start us, length us, event | category | flops | bytes accessed | tf_op | source)
XLA Modules:
  0.0 105.5 jit_solution(15692243112616137906)
XLA Ops:
  0.0 1.4 %multiply_add_fusion = s32[8192]{0:T(1024)} fusion(s32[8192]{0:T(1024)} %param.17, s32[8192]{0:T(1024)} %param.18), kind=kLoop, calls=%fused_computation.14 | loop fusion | flops 16384 | bytes 98304 | tf_op jit(solution)/shard_map/add | solution.py:375
  1.4 13.0 %binning.1 = f32[1024,128]{1,0:T(8,128)} custom-call(s32[1]{0:T(128)} %bitcast.pulse_base, f32[1,8192]{1,0:T(1,128)} %bitcast.39, f32[2,8192]{1,0:T(2,128)} %amp.1, s32[1,8192]{1,0:T(1,128)} %bitcast.38, s32[1,8192]{1,0:T(1,128)} %bitcast.37), custom_call_target="tpu_custom_call" | custom-call | tf_op jit(solution)/shard_map/binning/pallas_call | solution.py:113
  14.4 1.0 dynamic-slice_bitcast_fusion
  15.4 0.1 collective-permute-start
  15.5 0.8 stack_reshape.4
  16.4 0.1 sub.37
  16.6 0.4 collective-permute-done
  17.0 1.7 %bitcast_add_fusion.1 = f32[512,128]{1,0:T(8,128)} fusion(f32[512,128]{1,0:T(8,128)S(1)} %collective-permute-done, f32[2,512,128]{2,1,0:T(8,128)} %bitcast.35, s32[]{:T(128)S(6)} %select_n.27), kind=kLoop, calls=%fused_computation.11 | loop fusion | flops 65536 | bytes 786436 | tf_op jit(solution)/shard_map/add | solution.py:384
  18.7 6.7 %all-to-all-start = ((f32[8,64,128]{2,1,0:T(8,128)}), f32[8,64,128]{2,1,0:T(8,128)S(1)}, u32[]{:S(2)}, u32[]{:S(2)}) async-start(f32[8,64,128]{2,1,0:T(8,128)} %bitcast.7), calls=%async_computation | async-start | bytes 524288 | tf_op jit(solution)/shard_map/all_to_all | solution.py:386
  25.3 0.1 broadcast_add_fusion
  25.5 0.1 eq.19
  25.5 1.3 %copy.20.kind = s32[8,256,1]{2,1,0:T(8,128)} copy(s32[8,256,1]{1,0,2:T(8,128)S(1)} %add_bitcast_fusion) | data formatting | bytes 16384 | tf_op jit(solution)/shard_map/reshape | solution.py:366
  26.9 3.6 %fusion.4 = (f32[1024,128]{1,0:T(8,128)}, f32[1024,128]{1,0:T(8,128)}) fusion(f32[32,128]{1,0:T(8,128)S(1)} %get-tuple-element.13, f32[1024]{0:T(1024)S(1)} %sub.37, f32[32,128]{1,0:T(8,128)S(1)} %get-tuple-element.14, f32[1024]{0:T(1024)S(1)} %div.14), kind=kLoop, calls=%fused_computation.9 | loop fusion | flops 393216 | bytes 1089536 | tf_op jit(solution)/shard_map/sin | solution.py:373
  30.5 2.6 %all-to-all-done.x = f32[8,64,128]{2,1,0:T(8,128)S(1)} async-done(((f32[8,64,128]{2,1,0:T(8,128)}), f32[8,64,128]{2,1,0:T(8,128)S(1)}, u32[]{:S(2)}, u32[]{:S(2)}) %all-to-all-start) | async-done | bytes 262176 | tf_op jit(solution)/shard_map/all_to_all | solution.py:386
  33.1 0.7 copy-done.2
  33.8 2.6 %azimuth.1 = f32[16,4,8,128]{3,2,1,0:T(8,128)} custom-call(f32[8,64,128]{2,1,0:T(8,128)} %copy-done.2, bf16[2,4,256,128]{3,2,1,0:T(8,128)(2,1)} %constant.84.clone.table), custom_call_target="tpu_custom_call" | custom-call | tf_op jit(solution)/shard_map/azimuth/pallas_call | solution.py:393
  36.3 5.8 %all-to-all-start.1 = ((f32[16,4,8,128]{3,2,1,0:T(8,128)}), f32[16,4,8,128]{3,2,1,0:T(8,128)S(1)}, u32[]{:S(2)}, u32[]{:S(2)}) async-start(f32[16,4,8,128]{3,2,1,0:T(8,128)} %azimuth.1), calls=%async_computation.1 | async-start | bytes 524288 | tf_op jit(solution)/shard_map/all_to_all | solution.py:398
  42.1 1.1 %fusion.1.hot = bf16[8,256,128]{2,1,0:T(8,128)(2,1)} fusion(s32[8,256]{1,0:T(8,128)S(1)} %eq.19), kind=kLoop, calls=%fused_computation.4 | loop fusion | flops 524288 | bytes 532480 | tf_op jit(solution)/shard_map/convert_element_type | solution.py:365
  43.2 1.9 %fusion = (bf16[16,256,128]{2,1,0:T(8,128)(2,1)}, bf16[16,256,128]{2,1,0:T(8,128)(2,1)}) fusion(f32[16,256,128]{2,1,0:T(8,128)S(1)} %copy-done), kind=kLoop, calls=%fused_computation.2 | loop fusion | flops 2097152 | bytes 4194304 | tf_op jit(solution)/shard_map/convert_element_type | solution.py:368
  45.1 6.5 %all-to-all-done.1 = f32[16,4,8,128]{3,2,1,0:T(8,128)S(1)} async-done(((f32[16,4,8,128]{3,2,1,0:T(8,128)}), f32[16,4,8,128]{3,2,1,0:T(8,128)S(1)}, u32[]{:S(2)}, u32[]{:S(2)}) %all-to-all-start.1) | async-done | bytes 262176 | tf_op jit(solution)/shard_map/all_to_all | solution.py:398
  51.6 0.7 copy-done.1
  52.3 19.4 %middle.1 = f32[256,8,128]{2,1,0:T(8,128)} custom-call(f32[64,8,128]{2,1,0:T(8,128)} %bitcast.36, f32[1024,128]{1,0:T(8,128)} %get-tuple-element.10.cos_p, f32[1024,128]{1,0:T(8,128)} %get-tuple-element.9.sin_p, bf16[8,256,128]{2,1,0:T(8,128)(2,1)} %fusion.1.hot, s32[8,256,1]{2,1,0:T(8,128)} %copy.20.kind, bf16[16,256,128]{2,1,0:T(8,128)(2,1)} %get-tuple-element.8.bank_hi, ...), custom_call_target="tpu_custom_call" | custom-call | tf_op jit(solution)/shard_map/middle/pallas_call | solution.py:225
  71.7 30.1 %all_to_all.15.x = f32[16,2,8,8,128]{4,3,2,1,0:T(8,128)} all-to-all(f32[16,2,8,8,128]{4,3,2,1,0:T(8,128)} %bitcast.33), channel_id=1, replica_groups=mesh['scene'=2,'pulse'=8,'scat'=2] {'pulse','scat'}, dimensions={0} | all-to-all | bytes 2097152 | tf_op jit(solution)/shard_map/all_to_all | solution.py:425
  101.8 3.7 %image.1 = f32[2,512,256]{2,1,0:T(8,128)} custom-call(f32[16,2,8,8,128]{4,3,2,1,0:T(8,128)} %all_to_all.15.x, bf16[2,4,256,128]{3,2,1,0:T(8,128)(2,1)} %constant.85.clone.table), custom_call_target="tpu_custom_call" | custom-call | tf_op jit(solution)/shard_map/image/pallas_call | solution.py:428
  (15 shorter events, 0.3 us)
Async XLA Ops:
  0.0 25.3 %copy-start.3 = (s32[32,32]{1,0:T(8,128)S(1)}, s32[32,32]{1,0:T(8,128)}, u32[]{:S(2)}) copy-start(s32[32,32]{1,0:T(8,128)} %param.19) | copy-start | bytes 12292
  15.4 1.6 %collective-permute-start = (f32[512,128]{1,0:T(8,128)S(1)}, f32[512,128]{1,0:T(8,128)S(1)}, u32[]{:S(2)}, u32[]{:S(2)}) collective-permute-start(f32[512,128]{1,0:T(8,128)S(1)} %dynamic-slice_bitcast_fusion), channel_id=1, source_target_pairs={{0,1},{1,0},{2,3},{3,2},{4,5},{5,4},{6,7},{7,6},{8,9},{9,8},{10,11... | collective-permute-start | bytes 786440 | tf_op jit(solution)/shard_map/ppermute | solution.py:384
  18.7 14.4 %all-to-all-start = ((f32[8,64,128]{2,1,0:T(8,128)}), f32[8,64,128]{2,1,0:T(8,128)S(1)}, u32[]{:S(2)}, u32[]{:S(2)}) async-start(f32[8,64,128]{2,1,0:T(8,128)} %bitcast.7), calls=%async_computation | async-start | bytes 524288 | tf_op jit(solution)/shard_map/all_to_all | solution.py:386
  25.5 17.7 %copy-start = (f32[16,256,128]{2,1,0:T(8,128)S(1)}, f32[16,256,128]{2,1,0:T(8,128)}, u32[]{:S(2)}) copy-start(f32[16,256,128]{2,1,0:T(8,128)} %param.21) | copy-start | bytes 6291460
  33.1 0.7 copy-start.2
  36.3 15.3 %all-to-all-start.1 = ((f32[16,4,8,128]{3,2,1,0:T(8,128)}), f32[16,4,8,128]{3,2,1,0:T(8,128)S(1)}, u32[]{:S(2)}, u32[]{:S(2)}) async-start(f32[16,4,8,128]{3,2,1,0:T(8,128)} %azimuth.1), calls=%async_computation.1 | async-start | bytes 524288 | tf_op jit(solution)/shard_map/all_to_all | solution.py:398
  51.6 0.7 copy-start.1

commit v3 on v2

--- a/solution.py
+++ b/solution.py
@@ -73,7 +73,7 @@
     base = pulse_base[0]
     ids = base + lax.broadcasted_iota(jnp.int32, (pulses, width), 0)
     along = (ids.astype(f32) - P_SIZE // 2) * SPACING
-    target = tgt[...]
+    target = tgt[...] + SHIFT * bnc[...]
     slant = NEAR + target.astype(f32)
     offset = along - pos[...]
     square = offset * offset
@@ -105,9 +105,9 @@
         out[...] = acc[:, : 2 * pulses] + acc[:, 2 * pulses :]
 
 
-def binning(positions, amplitude, target, bounce, pulse_base, pulses):
+def binning(positions, amplitude, cells, bounce, pulse_base, pulses):
     count = positions.shape[0]
-    width = min(512, count)
+    width = min(2048, count)
     sin_c, cos_c = trig_coefs()
     row = lambda n: pl.BlockSpec((n, width), lambda i: (0, i))
     return pl.pallas_call(
@@ -122,7 +122,7 @@
         pulse_base.reshape(1),
         positions.reshape(1, count),
         amplitude,
-        target.reshape(1, count),
+        cells.reshape(1, count),
         bounce.reshape(1, count),
     )
 
@@ -219,7 +219,7 @@
 
 def middle(x, cos_p, sin_p, hot, kind, bank_hi, bank_lo, tables):
     groups = x.shape[1]
-    subs = min(2, groups)
+    subs = min(4, groups)
     n = GROUP * BLOCKS
     whole = lambda a: pl.BlockSpec(a.shape, lambda i: (0,) * a.ndim)
     return pl.pallas_call(
@@ -372,8 +372,7 @@
     theta = theta.reshape(rows * BLOCKS, STOLT)
     cos_p, sin_p = jnp.cos(theta), jnp.sin(theta)
 
-    target = range_cells + SHIFT * bounce
-    partial = binning(positions, amplitude, target, bounce, pulse_here * pulses, pulses)
+    partial = binning(positions, amplitude, range_cells, bounce, pulse_here * pulses, pulses)
     partial = partial.reshape(n_scat, bins_scat, 2 * pulses)
     binned = lax.dynamic_index_in_dim(partial, scat_here, 0, keepdims=False)
     for shift in range(1, n_scat):

time: 107 us -> 102 us (0.953)
  Pallas kernels: 38.8 us -> 35.7 us
  other arithmetic: 9.75 us -> 8.35 us
    pallas_call x1, Pallas kernels: 13 us -> 10.2 us  [binning(): pl.pallas_call(functools.partial(bin_kernel, pulses=pulses, sin_c=sin_c,...]
    add x1 -> x0, other arithmetic: 1.4 us -> none  [on_device(): target = range_cells + SHIFT * bounce]
where the time goes in v3:
time: 102 us; the launch traced here: 101 us
  Pallas kernels  35.7 us (35%)
  blocking collectives  30.1 us (30%)
  starting transfers between devices  12.5 us (12%)
  waiting for transfers between devices  9.51 us (9%)
  other arithmetic  8.35 us (8%)
  local copies, waits for them, and re-layouts  4.9 us (5%)
    all_to_all x1, blocking collectives, on_device(): lax.all_to_all(ranged.reshape(n_dev, 2, per, groups, n), ('pulse', 'scat'...  30.1 us
    pallas_call x1, Pallas kernels, middle(): pl.pallas_call(functools.partial(mid_kernel, subs=subs), grid=(groups //...  19.2 us
    pallas_call x1, Pallas kernels, binning(): pl.pallas_call(functools.partial(bin_kernel, pulses=pulses, sin_c=sin_c,...  10.2 us
    all_to_all x1, starting transfers between devices, on_device(): lax.all_to_all(binned.reshape(n_pulse, bins_here, 2 * pulses), 'pulse', 0...  6.64 us
    all_to_all x1, waiting for transfers between devices, on_device(): x = lax.all_to_all(spectrum, ('pulse', 'scat'), 0, 0, tiled=True)  6.53 us
    all_to_all x1, starting transfers between devices, on_device(): x = lax.all_to_all(spectrum, ('pulse', 'scat'), 0, 0, tiled=True)  5.76 us
    pallas_call x1, Pallas kernels, on_device(): pl.pallas_call(image_kernel, out_shape=jax.ShapeDtypeStruct((2, P_SIZE, w...  3.74 us
    sin x1, other arithmetic, on_device(): cos_p, sin_p = (jnp.cos(theta), jnp.sin(theta))  3.58 us
  transfers between devices with their start and end apart: 3, of which 3 were waited for; matrix products, arithmetic and copies ran while one was open for 9% of the time, Pallas kernels for 0%

profile of v3, /device:TPU:1, one launch (start us, length us, event | category | flops | bytes accessed | tf_op | source)
XLA Modules:
  0.0 101.0 jit_solution(6336694947722260767)
XLA Ops:
  0.0 10.2 %binning.1 = f32[1024,128]{1,0:T(8,128)} custom-call(s32[1]{0:T(128)} %bitcast.pulse_base, f32[1,8192]{1,0:T(1,128)} %bitcast.37, f32[2,8192]{1,0:T(2,128)} %amp.1, s32[1,8192]{1,0:T(1,128)} %bitcast.38, s32[1,8192]{1,0:T(1,128)} %bitcast.39), custom_call_target="tpu_custom_call" | custom-call | tf_op jit(solution)/shard_map/binning/pallas_call | solution.py:113
  10.2 1.0 dynamic-slice_bitcast_fusion
  11.1 0.1 collective-permute-start
  11.2 0.8 stack_reshape.4
  12.1 0.1 sub.37
  12.2 0.1 div.14
  12.3 0.4 collective-permute-done
  12.7 1.7 %bitcast_add_fusion.1 = f32[512,128]{1,0:T(8,128)} fusion(f32[512,128]{1,0:T(8,128)S(1)} %collective-permute-done, f32[2,512,128]{2,1,0:T(8,128)} %bitcast.35, s32[]{:T(128)S(6)} %select_n.27), kind=kLoop, calls=%fused_computation.11 | loop fusion | flops 65536 | bytes 786436 | tf_op jit(solution)/shard_map/add | solution.py:383
  14.4 6.6 %all-to-all-start = ((f32[8,64,128]{2,1,0:T(8,128)}), f32[8,64,128]{2,1,0:T(8,128)S(1)}, u32[]{:S(2)}, u32[]{:S(2)}) async-start(f32[8,64,128]{2,1,0:T(8,128)} %bitcast.7), calls=%async_computation | async-start | bytes 524288 | tf_op jit(solution)/shard_map/all_to_all | solution.py:385
  21.1 0.1 broadcast_add_fusion
  21.2 0.1 eq.19
  21.2 1.3 %copy.20.kind = s32[8,256,1]{2,1,0:T(8,128)} copy(s32[8,256,1]{1,0,2:T(8,128)S(1)} %add_bitcast_fusion) | data formatting | bytes 16384 | tf_op jit(solution)/shard_map/reshape | solution.py:366
  22.6 3.6 %fusion.4 = (f32[1024,128]{1,0:T(8,128)}, f32[1024,128]{1,0:T(8,128)}) fusion(f32[32,128]{1,0:T(8,128)S(1)} %get-tuple-element.13, f32[1024]{0:T(1024)S(1)} %sub.37, f32[32,128]{1,0:T(8,128)S(1)} %get-tuple-element.14, f32[1024]{0:T(1024)S(1)} %div.14), kind=kLoop, calls=%fused_computation.9 | loop fusion | flops 393216 | bytes 1089536 | tf_op jit(solution)/shard_map/sin | solution.py:373
  26.2 2.6 %all-to-all-done.x = f32[8,64,128]{2,1,0:T(8,128)S(1)} async-done(((f32[8,64,128]{2,1,0:T(8,128)}), f32[8,64,128]{2,1,0:T(8,128)S(1)}, u32[]{:S(2)}, u32[]{:S(2)}) %all-to-all-start) | async-done | bytes 262176 | tf_op jit(solution)/shard_map/all_to_all | solution.py:385
  28.8 0.7 copy-done.2
  29.5 2.6 %azimuth.1 = f32[16,4,8,128]{3,2,1,0:T(8,128)} custom-call(f32[8,64,128]{2,1,0:T(8,128)} %copy-done.2, bf16[2,4,256,128]{3,2,1,0:T(8,128)(2,1)} %constant.82.clone.table), custom_call_target="tpu_custom_call" | custom-call | tf_op jit(solution)/shard_map/azimuth/pallas_call | solution.py:392
  32.0 5.8 %all-to-all-start.1 = ((f32[16,4,8,128]{3,2,1,0:T(8,128)}), f32[16,4,8,128]{3,2,1,0:T(8,128)S(1)}, u32[]{:S(2)}, u32[]{:S(2)}) async-start(f32[16,4,8,128]{3,2,1,0:T(8,128)} %azimuth.1), calls=%async_computation.1 | async-start | bytes 524288 | tf_op jit(solution)/shard_map/all_to_all | solution.py:397
  37.8 1.1 %fusion.1.hot = bf16[8,256,128]{2,1,0:T(8,128)(2,1)} fusion(s32[8,256]{1,0:T(8,128)S(1)} %eq.19), kind=kLoop, calls=%fused_computation.4 | loop fusion | flops 524288 | bytes 532480 | tf_op jit(solution)/shard_map/convert_element_type | solution.py:365
  38.9 1.9 %fusion = (bf16[16,256,128]{2,1,0:T(8,128)(2,1)}, bf16[16,256,128]{2,1,0:T(8,128)(2,1)}) fusion(f32[16,256,128]{2,1,0:T(8,128)S(1)} %copy-done), kind=kLoop, calls=%fused_computation.2 | loop fusion | flops 2097152 | bytes 4194304 | tf_op jit(solution)/shard_map/convert_element_type | solution.py:368
  40.8 6.5 %all-to-all-done.1 = f32[16,4,8,128]{3,2,1,0:T(8,128)S(1)} async-done(((f32[16,4,8,128]{3,2,1,0:T(8,128)}), f32[16,4,8,128]{3,2,1,0:T(8,128)S(1)}, u32[]{:S(2)}, u32[]{:S(2)}) %all-to-all-start.1) | async-done | bytes 262176 | tf_op jit(solution)/shard_map/all_to_all | solution.py:397
  47.3 0.7 copy-done.1
  48.0 19.2 %middle.1 = f32[256,8,128]{2,1,0:T(8,128)} custom-call(f32[64,8,128]{2,1,0:T(8,128)} %bitcast.36, f32[1024,128]{1,0:T(8,128)} %get-tuple-element.10.cos_p, f32[1024,128]{1,0:T(8,128)} %get-tuple-element.9.sin_p, bf16[8,256,128]{2,1,0:T(8,128)(2,1)} %fusion.1.hot, s32[8,256,1]{2,1,0:T(8,128)} %copy.20.kind, bf16[16,256,128]{2,1,0:T(8,128)(2,1)} %get-tuple-element.8.bank_hi, ...), custom_call_target="tpu_custom_call" | custom-call | tf_op jit(solution)/shard_map/middle/pallas_call | solution.py:225
  67.2 30.1 %all_to_all.15.x = f32[16,2,8,8,128]{4,3,2,1,0:T(8,128)} all-to-all(f32[16,2,8,8,128]{4,3,2,1,0:T(8,128)} %bitcast.33), channel_id=1, replica_groups=mesh['scene'=2,'pulse'=8,'scat'=2] {'pulse','scat'}, dimensions={0} | all-to-all | bytes 2097152 | tf_op jit(solution)/shard_map/all_to_all | solution.py:424
  97.3 3.7 %image.1 = f32[2,512,256]{2,1,0:T(8,128)} custom-call(f32[16,2,8,8,128]{4,3,2,1,0:T(8,128)} %all_to_all.15.x, bf16[2,4,256,128]{3,2,1,0:T(8,128)(2,1)} %constant.83.clone.table), custom_call_target="tpu_custom_call" | custom-call | tf_op jit(solution)/shard_map/image/pallas_call | solution.py:427
  (14 shorter events, 0.2 us)
Async XLA Ops:
  0.0 21.0 %copy-start.3 = (s32[32,32]{1,0:T(8,128)S(1)}, s32[32,32]{1,0:T(8,128)}, u32[]{:S(2)}) copy-start(s32[32,32]{1,0:T(8,128)} %param.19) | copy-start | bytes 12292
  11.1 1.6 %collective-permute-start = (f32[512,128]{1,0:T(8,128)S(1)}, f32[512,128]{1,0:T(8,128)S(1)}, u32[]{:S(2)}, u32[]{:S(2)}) collective-permute-start(f32[512,128]{1,0:T(8,128)S(1)} %dynamic-slice_bitcast_fusion), channel_id=1, source_target_pairs={{0,1},{1,0},{2,3},{3,2},{4,5},{5,4},{6,7},{7,6},{8,9},{9,8},{10,11... | collective-permute-start | bytes 786440 | tf_op jit(solution)/shard_map/ppermute | solution.py:383
  14.4 14.4 %all-to-all-start = ((f32[8,64,128]{2,1,0:T(8,128)}), f32[8,64,128]{2,1,0:T(8,128)S(1)}, u32[]{:S(2)}, u32[]{:S(2)}) async-start(f32[8,64,128]{2,1,0:T(8,128)} %bitcast.7), calls=%async_computation | async-start | bytes 524288 | tf_op jit(solution)/shard_map/all_to_all | solution.py:385
  21.2 17.7 %copy-start = (f32[16,256,128]{2,1,0:T(8,128)S(1)}, f32[16,256,128]{2,1,0:T(8,128)}, u32[]{:S(2)}) copy-start(f32[16,256,128]{2,1,0:T(8,128)} %param.21) | copy-start | bytes 6291460
  28.8 0.7 copy-start.2
  32.0 15.3 %all-to-all-start.1 = ((f32[16,4,8,128]{3,2,1,0:T(8,128)}), f32[16,4,8,128]{3,2,1,0:T(8,128)S(1)}, u32[]{:S(2)}, u32[]{:S(2)}) async-start(f32[16,4,8,128]{3,2,1,0:T(8,128)} %azimuth.1), calls=%async_computation.1 | async-start | bytes 524288 | tf_op jit(solution)/shard_map/all_to_all | solution.py:397
  47.3 0.7 copy-start.1
